TPU v7x, 32 devices: a whole 2x2x4 slice. The times are simulated.
32 devices in a mesh: head: 8 (over y, x, core), seq: 4 (over z).
Axes of the slice: x: 2, y: 2, z: 4, core: 2. Of those that a mesh axis runs over, the one named last changes fastest.
Arguments:
- query_rows: bfloat16 [512, 16384], P('seq', 'head'), may hold values from -512 to 512
- key_rows: bfloat16 [512, 1024], P('seq'), may hold values from -32 to 32
- value_rows: bfloat16 [512, 1024], P('seq'), may hold values from -6 to 6
- positions: int32 [512], P('seq'), may hold values from 0 to 511, as said below
Outputs:
- attended: bfloat16 [512, 16384], P('seq', 'head')
- hessian: float32 [16384, 16384], P('head', 'seq')
Inputs may be any that keep to these rules, and one draw needn't show every extreme that they name: Each aligned block of 4 spans of 128 tokens is one sequence; each span holds 128 consecutive ascending positions starting at a multiple of 128, and the sequence's spans together hold every position 0 to 511 once.
All inputs are finite; a program needn't handle non-finite values.
Results may differ from a plain program's by a relative error of at most 0.0037.
Values may be sent and summed in bfloat16 or wider, within the bound.
A program may use at most 128 MiB of HBM per device.

v0:
```python
import functools

import jax
import jax.numpy as jnp
from jax import lax
from jax.experimental import pallas as pl
from jax.experimental.pallas import tpu as pltpu
from jax.sharding import PartitionSpec as P

HEADS = 128
KVH = 8
HD = 128
SPANS = 4
CHUNK_HEADS = 4
TILE = 512
MESH = pl.DeviceIdType.MESH


def exchange_kernel(
    seq_devices, head_devices, chunks,
    q_ref, k_ref, v_ref, pos_ref, attended_ref, turned_ref, cols_ref,
    rows_ref, kbuf, vbuf, pbuf,
    kv_send, kv_recv, line_send, line_recv, tree_send, tree_recv, lane_send, lane_recv,
):
    tokens, width = q_ref.shape
    lanes = head_devices // seq_devices
    bits = seq_devices.bit_length() - 1
    chunk_width = width // chunks
    chunk_heads = chunk_width // HD
    score_scale = HD ** (-0.5)
    head = lax.axis_index("head")
    span = lax.axis_index("seq")
    node, lane = head // lanes, head % lanes
    group = (span // SPANS) * SPANS
    place = span % SPANS

    def flip(bit):
        has = (node // 2**bit) % 2
        return (node + (1 - 2 * has) * 2**bit) * lanes + lane

    far = [(node // 2**bit + span // 2**bit) % 2 for bit in range(bits)]
    above = [sum(far[bit:]) for bit in range(bits)]
    below = [sum(far[: bit + 1]) for bit in range(bits)]
    root = above[0] == 0
    not_root = above[0] > 0

    def peer(step):
        return group + (place + step) % SPANS

    def mate(step):
        return node * lanes + (lane + step) % lanes

    barrier = pltpu.get_barrier_semaphore()
    count = 0
    for step in range(1, SPANS):
        pl.semaphore_signal(barrier, inc=1, device_id={"seq": peer(step)}, device_id_type=MESH)
        count += 1
    for bit in range(bits):
        pl.semaphore_signal(barrier, inc=1, device_id={"head": flip(bit)}, device_id_type=MESH)
        count += 1
    for step in range(1, lanes):
        pl.semaphore_signal(barrier, inc=1, device_id={"head": mate(step)}, device_id_type=MESH)
        count += 1
    if seq_devices > SPANS:
        @pl.when(span > 0)
        def _():
            pl.semaphore_signal(barrier, inc=1, device_id={"seq": span - 1}, device_id_type=MESH)

        @pl.when(span < seq_devices - 1)
        def _():
            pl.semaphore_signal(barrier, inc=1, device_id={"seq": span + 1}, device_id_type=MESH)

        @pl.when(span > 0)
        def _():
            pl.semaphore_wait(barrier, 1)

        @pl.when(span < seq_devices - 1)
        def _():
            pl.semaphore_wait(barrier, 1)

    pl.semaphore_wait(barrier, count)
    key_head = head * (width // HD) // (HEADS // KVH)
    key_columns = pl.ds(pl.multiple_of(key_head * HD, HD), HD)

    def kv_copies(step):
        copies = []
        for which, (src, dst) in enumerate((
            (k_ref.at[:, key_columns], kbuf.at[place]),
            (v_ref.at[:, key_columns], vbuf.at[place]),
            (pos_ref, pbuf.at[place]),
        )):
            copies.append(pltpu.make_async_remote_copy(
                src_ref=src, dst_ref=dst,
                send_sem=kv_send.at[which, step - 1], recv_sem=kv_recv.at[which, step - 1],
                device_id={"seq": peer(step)}, device_id_type=MESH,
            ))
        return copies

    def kv_arrivals(step):
        source = (place + SPANS - step) % SPANS
        copies = []
        for which, (src, dst) in enumerate((
            (k_ref.at[:, key_columns], kbuf.at[source]),
            (v_ref.at[:, key_columns], vbuf.at[source]),
            (pos_ref, pbuf.at[source]),
        )):
            copies.append(pltpu.make_async_remote_copy(
                src_ref=src, dst_ref=dst,
                send_sem=kv_send.at[which, step - 1], recv_sem=kv_recv.at[which, step - 1],
                device_id={"seq": peer(step)}, device_id_type=MESH,
            ))
        return copies

    for step in range(1, SPANS):
        for copy in kv_copies(step):
            copy.start()
    kbuf[place] = k_ref[:, key_columns]
    vbuf[place] = v_ref[:, key_columns]
    pbuf[place] = pos_ref[...]

    def row_chunk(block, part):
        return (
            pl.ds(pl.multiple_of(block * tokens, tokens), tokens),
            pl.ds(pl.multiple_of(part * chunk_width, chunk_width), chunk_width),
        )

    def col_chunk(of_lane, block, part):
        return (
            pl.ds(pl.multiple_of(block * tokens, tokens), tokens),
            pl.ds(pl.multiple_of(of_lane * width + part * chunk_width, chunk_width), chunk_width),
        )

    def line_copy(way, block, part):
        where = rows_ref.at[row_chunk(block, part)]
        return pltpu.make_async_remote_copy(
            src_ref=where, dst_ref=where,
            send_sem=line_send.at[way, block, part], recv_sem=line_recv.at[block, part],
            device_id={"seq": span + 1 - 2 * way}, device_id_type=MESH,
        )

    def tree_copy(bit, block, part, source):
        return pltpu.make_async_remote_copy(
            src_ref=source, dst_ref=cols_ref.at[col_chunk(lane, block, part)],
            send_sem=tree_send.at[bit, block, part], recv_sem=tree_recv.at[block, part],
            device_id={"head": flip(bit)}, device_id_type=MESH,
        )

    def lane_copy(step, of_lane, block, part, source):
        return pltpu.make_async_remote_copy(
            src_ref=source, dst_ref=cols_ref.at[col_chunk(of_lane, block, part)],
            send_sem=lane_send.at[step - 1, block, part],
            recv_sem=lane_recv.at[step - 1, block, part],
            device_id={"head": mate(step)}, device_id_type=MESH,
        )

    def sends(bit, block, part):
        turn = (block + part) % 2
        return turn * above[bit] + (1 - turn) * below[bit] == 0

    def spread(block, part, source):
        for bit in range(bits):
            @pl.when(sends(bit, block, part))
            def _():
                tree_copy(bit, block, part, source).start()
        for step in range(1, lanes):
            lane_copy(step, lane, block, part, source).start()

    def on_row(block, part, up, down):
        @pl.when(up)
        def _():
            line_copy(0, block, part).start()

        @pl.when(down)
        def _():
            line_copy(1, block, part).start()

        @pl.when(root)
        def _():
            spread(block, part, rows_ref.at[row_chunk(block, part)])
            cols_ref[col_chunk(lane, block, part)] = rows_ref[row_chunk(block, part)]

        turned_ref[
            pl.ds(pl.multiple_of(part * chunk_width, chunk_width), chunk_width),
            pl.ds(pl.multiple_of(block * tokens, tokens), tokens),
        ] = rows_ref[row_chunk(block, part)].T

    has_up = span < seq_devices - 1
    has_down = span > 0

    for step in range(1, SPANS):
        for copy in kv_arrivals(step):
            copy.wait_recv()

    keys = kbuf[...].reshape(SPANS * tokens, HD)
    values = vbuf[...].reshape(SPANS * tokens, HD)
    key_places = jnp.concatenate([pbuf[j] for j in range(SPANS)], axis=1)
    query_places = jnp.broadcast_to(pos_ref[0:1, 0:1], (tokens, 1)) + lax.broadcasted_iota(
        jnp.int32, (tokens, 1), 0
    )
    visible = key_places <= query_places

    def compute(part, carry):
        pieces = []
        for h in range(chunk_heads):
            columns = pl.ds(pl.multiple_of(part * chunk_width + h * HD, HD), HD)
            queries = q_ref[:, columns]
            scores = lax.dot_general(
                queries, keys, (((1,), (1,)), ((), ())), preferred_element_type=jnp.float32
            ) * score_scale
            masked = jnp.where(visible, scores, -jnp.inf)
            row_top = jnp.max(masked, axis=1, keepdims=True)
            weights = jnp.exp(masked - row_top)
            weight_sum = jnp.sum(weights, axis=1, keepdims=True)
            mixed = jnp.dot(
                weights.astype(jnp.bfloat16), values, preferred_element_type=jnp.float32
            )
            pieces.append((mixed / weight_sum).astype(jnp.bfloat16))
        joined = jnp.concatenate(pieces, axis=1)
        rows_ref[row_chunk(span, part)] = joined
        attended_ref[:, pl.ds(pl.multiple_of(part * chunk_width, chunk_width), chunk_width)] = joined

        on_row(span, part, has_up, has_down)
        return carry

    lax.fori_loop(0, chunks, compute, 0)

    def relay(item, carry):
        back, part = item // chunks, item % chunks
        reach = back + 1

        @pl.when(reach <= span)
        def _():
            block = span - reach
            line_copy(0, block, part).wait_recv()
            on_row(block, part, has_up, False)

        @pl.when(span + reach < seq_devices)
        def _():
            block = span + reach
            line_copy(1, block, part).wait_recv()
            on_row(block, part, False, has_down)

        @pl.when(jnp.logical_and(not_root, item >= chunks))
        def _():
            late = back - 1

            def from_parent(block):
                source = cols_ref.at[col_chunk(lane, block, part)]
                tree_copy(0, block, part, source).wait_recv()
                spread(block, part, source)

            @pl.when(late <= span)
            def _():
                from_parent(span - late)

            @pl.when(jnp.logical_and(late > 0, span + late < seq_devices))
            def _():
                from_parent(span + late)

        return carry

    lax.fori_loop(0, (seq_devices + 1) * chunks, relay, 0)

    def drain(item, carry):
        block, part = item // chunks, item % chunks
        source = cols_ref.at[col_chunk(lane, block, part)]

        @pl.when(jnp.logical_and(has_up, block <= span))
        def _():
            line_copy(0, block, part).wait_send()

        @pl.when(jnp.logical_and(has_down, block >= span))
        def _():
            line_copy(1, block, part).wait_send()

        for bit in range(bits):
            @pl.when(sends(bit, block, part))
            def _():
                tree_copy(bit, block, part, source).wait_send()
        for step in range(1, lanes):
            lane_copy(step, lane, block, part, source).wait_send()
            lane_copy(step, (lane + lanes - step) % lanes, block, part, source).wait_recv()
        return carry

    lax.fori_loop(0, seq_devices * chunks, drain, 0)

    for step in range(1, SPANS):
        for copy in kv_copies(step):
            copy.wait_send()


def hessian_kernel(own_ref, turned_ref, cols_ref, attended_ref, out_ref):
    @pl.when(pl.program_id(0) == 0)
    def _():
        attended_ref[...] = own_ref[...]

    out_ref[...] = jnp.dot(turned_ref[...], cols_ref[...], preferred_element_type=jnp.float32)


def on_device(query_rows, key_rows, value_rows, positions):
    tokens, width = query_rows.shape
    seq_devices = lax.axis_size("seq")
    head_devices = lax.axis_size("head")
    lanes = head_devices // seq_devices
    bits = seq_devices.bit_length() - 1
    chunks = max(1, width // (CHUNK_HEADS * HD))
    vmem = pl.BlockSpec(memory_space=pltpu.VMEM)
    dma = pltpu.SemaphoreType.DMA
    own, turned, cols = pl.pallas_call(
        functools.partial(exchange_kernel, seq_devices, head_devices, chunks),
        out_shape=(
            jax.ShapeDtypeStruct((tokens, width), jnp.bfloat16),
            jax.ShapeDtypeStruct((width, seq_devices * tokens), jnp.bfloat16),
            jax.ShapeDtypeStruct((seq_devices * tokens, lanes * width), jnp.bfloat16),
        ),
        in_specs=[vmem] * 4,
        out_specs=(vmem, vmem, vmem),
        scratch_shapes=[
            pltpu.VMEM((seq_devices * tokens, width), jnp.bfloat16),
            pltpu.VMEM((SPANS, tokens, HD), jnp.bfloat16),
            pltpu.VMEM((SPANS, tokens, HD), jnp.bfloat16),
            pltpu.VMEM((SPANS, 1, tokens), jnp.int32),
            dma((3, SPANS - 1)),
            dma((3, SPANS - 1)),
            dma((2, seq_devices, chunks)),
            dma((seq_devices, chunks)),
            dma((bits, seq_devices, chunks)),
            dma((seq_devices, chunks)),
            dma((lanes - 1, seq_devices, chunks)),
            dma((lanes - 1, seq_devices, chunks)),
        ],
        compiler_params=pltpu.CompilerParams(collective_id=0, has_side_effects=True),
        name="attend_exchange",
    )(query_rows, key_rows, value_rows, positions.reshape(1, tokens))
    depth, breadth = cols.shape
    tile = min(TILE, breadth)
    attended, hessian = pl.pallas_call(
        hessian_kernel,
        grid=(breadth // tile,),
        out_shape=(
            jax.ShapeDtypeStruct((tokens, width), jnp.bfloat16),
            jax.ShapeDtypeStruct((width, breadth), jnp.float32),
        ),
        in_specs=[
            pl.BlockSpec((tokens, width), lambda j: (0, 0)),
            pl.BlockSpec((width, depth), lambda j: (0, 0)),
            pl.BlockSpec((depth, tile), lambda j: (0, j)),
        ],
        out_specs=(
            pl.BlockSpec((tokens, width), lambda j: (0, 0)),
            pl.BlockSpec((width, tile), lambda j: (0, j)),
        ),
        name="hessian",
    )(own, turned, cols)
    return (attended, hessian)


def solution(mesh):
    placed = (P("seq", "head"), P("seq", None), P("seq", None), P("seq"))
    return jax.shard_map(
        on_device,
        mesh=mesh,
        in_specs=placed,
        out_specs=(P("seq", "head"), P("head", "seq")),
        check_vma=False,
    )
```

profile of v0, /device:TPU:25, one launch (start us, length us, event | category | flops | bytes accessed | tf_op | source)
XLA Modules:
  0.0 84.4 jit_solution(6724036176352421750)
XLA Ops:
  0.6 67.4 %attend_exchange.1 = (bf16[128,2048]{1,0:T(8,128)(2,1)}, bf16[2048,512]{1,0:T(8,128)(2,1)}, bf16[512,4096]{1,0:T(8,128)(2,1)}) custom-call(bf16[128,2048]{1,0:T(8,128)(2,1)} %q_ref.1, bf16[128,1024]{1,0:T(8,128)(2,1)} %k_ref.1, bf16[128,1024]{1,0:T(8,128)(2,1)} %v_ref.1, s32[1,128]{1,0:T(1,128)} %bitcast.1), custom_call_target="tpu_custom_call" | custom-call | tf_op jit(solution)/shard_map/attend_exchange/pallas_call | solution.py:309
  68.0 16.4 %hessian.1 = (bf16[128,2048]{1,0:T(8,128)(2,1)}, f32[2048,4096]{1,0:T(8,128)}) custom-call(bf16[128,2048]{1,0:T(8,128)(2,1)} %get-tuple-element.5.own_ref, bf16[2048,512]{1,0:T(8,128)(2,1)} %get-tuple-element.6.turned_ref, bf16[512,4096]{1,0:T(8,128)(2,1)} %get-tuple-element.7.cols_ref), custom_call_target="tpu_custom_call" | custom-call | tf_op jit(solution)/shard_map/hessian/pallas_call | solution.py:337
where the time goes:
time: 84.6 us; the launch traced here: 84.4 us
  Pallas kernels  83.7 us (99%)
    pallas_call x1, Pallas kernels, on_device(): pl.pallas_call(functools.partial(exchange_kernel, seq_devices, head_devic...  67.4 us
    pallas_call x1, Pallas kernels, on_device(): pl.pallas_call(hessian_kernel, grid=(breadth // tile,), out_shape=(jax.Sh...  16.4 us

commit v1 on v0

--- a/solution.py
+++ b/solution.py
@@ -11,8 +11,12 @@
 KVH = 8
 HD = 128
 SPANS = 4
-CHUNK_HEADS = 4
+CHUNK_HEADS = 2
+TREE_PARTS = 2
+LAG = 2
 TILE = 512
+SLOTS = 4
+VMEM_BYTES = 28 * 1024 * 1024
 MESH = pl.DeviceIdType.MESH
 
 
@@ -155,7 +159,16 @@
 
     def sends(bit, block, part):
         turn = (block + part) % 2
-        return turn * above[bit] + (1 - turn) * below[bit] == 0
+        count = turn * above[bit] + (1 - turn) * below[bit]
+        if bits == 2:
+            first, last = far[bit], far[1 - bit]
+            corner = (first - last) * (first - last)
+            middle = 1 - last * (1 - first)
+            starts = turn if bit == 1 else 1 - turn
+            walk = starts * corner + (1 - starts) * middle
+            early = jnp.where(part < chunks - TREE_PARTS, 1, 0)
+            count = early * walk + (1 - early) * count
+        return count == 0
 
     def spread(block, part, source):
         for bit in range(bits):
@@ -224,42 +237,66 @@
 
     lax.fori_loop(0, chunks, compute, 0)
 
+    if bits == 2:
+        depths = [
+            far[turn] * (1 + far[1 - turn]) + 3 * (1 - far[turn]) * far[1 - turn]
+            for turn in range(2)
+        ]
+        deepest = 3
+    else:
+        depths = [above[0], above[0]]
+        deepest = bits
+
     def relay(item, carry):
-        back, part = item // chunks, item % chunks
-        reach = back + 1
-
-        @pl.when(reach <= span)
+        reach, part = item // chunks, item % chunks
+        inside = jnp.logical_and(reach > 0, reach < seq_devices)
+
+        @pl.when(jnp.logical_and(inside, reach <= span))
         def _():
             block = span - reach
             line_copy(0, block, part).wait_recv()
             on_row(block, part, has_up, False)
 
-        @pl.when(span + reach < seq_devices)
+        @pl.when(jnp.logical_and(inside, span + reach < seq_devices))
         def _():
             block = span + reach
             line_copy(1, block, part).wait_recv()
             on_row(block, part, False, has_down)
 
-        @pl.when(jnp.logical_and(not_root, item >= chunks))
-        def _():
-            late = back - 1
-
-            def from_parent(block):
-                source = cols_ref.at[col_chunk(lane, block, part)]
-                tree_copy(0, block, part, source).wait_recv()
-                spread(block, part, source)
-
-            @pl.when(late <= span)
+        for turn in range(2):
+            late = item - LAG * depths[turn]
+            distance, piece = late // chunks, late % chunks
+            known = jnp.logical_and(not_root, late >= 0)
+
+            def from_parent(block, piece=piece):
+                source = cols_ref.at[col_chunk(lane, block, piece)]
+                tree_copy(0, block, piece, source).wait_recv()
+                spread(block, piece, source)
+
+            @pl.when(
+                jnp.logical_and(
+                    jnp.logical_and(known, distance <= span),
+                    (span + seq_devices - distance + piece + turn) % 2 == 0,
+                )
+            )
             def _():
-                from_parent(span - late)
-
-            @pl.when(jnp.logical_and(late > 0, span + late < seq_devices))
+                from_parent(span - distance)
+
+            @pl.when(
+                jnp.logical_and(
+                    jnp.logical_and(known, distance > 0),
+                    jnp.logical_and(
+                        span + distance < seq_devices,
+                        (span + distance + piece + turn) % 2 == 0,
+                    ),
+                )
+            )
             def _():
-                from_parent(span + late)
+                from_parent(span + distance)
 
         return carry
 
-    lax.fori_loop(0, (seq_devices + 1) * chunks, relay, 0)
+    lax.fori_loop(0, seq_devices * chunks + LAG * deepest, relay, 0)
 
     def drain(item, carry):
         block, part = item // chunks, item % chunks
@@ -289,12 +326,35 @@
             copy.wait_send()
 
 
-def hessian_kernel(own_ref, turned_ref, cols_ref, attended_ref, out_ref):
-    @pl.when(pl.program_id(0) == 0)
-    def _():
-        attended_ref[...] = own_ref[...]
-
-    out_ref[...] = jnp.dot(turned_ref[...], cols_ref[...], preferred_element_type=jnp.float32)
+def hessian_kernel(own_ref, turned_ref, cols_ref, attended_ref, out_ref, ring, own_sem, ring_sem):
+    tile = ring.shape[2]
+    slots = ring.shape[0]
+    tiles = out_ref.shape[1] // tile
+    own = pltpu.make_async_copy(own_ref, attended_ref, own_sem)
+    own.start()
+
+    def columns(j):
+        return pl.ds(pl.multiple_of(j * tile, tile), tile)
+
+    def put(j):
+        slot = j % slots
+        return pltpu.make_async_copy(ring.at[slot], out_ref.at[:, columns(j)], ring_sem.at[slot])
+
+    def body(j, carry):
+        @pl.when(j >= slots)
+        def _():
+            put(j - slots).wait()
+
+        ring[j % slots] = jnp.dot(
+            turned_ref[...], cols_ref[:, columns(j)], preferred_element_type=jnp.float32
+        )
+        put(j).start()
+        return carry
+
+    lax.fori_loop(0, tiles, body, 0)
+    for j in range(max(0, tiles - slots), tiles):
+        put(j).wait()
+    own.wait()
 
 
 def on_device(query_rows, key_rows, value_rows, positions):
@@ -329,27 +389,28 @@
             dma((lanes - 1, seq_devices, chunks)),
             dma((lanes - 1, seq_devices, chunks)),
         ],
-        compiler_params=pltpu.CompilerParams(collective_id=0, has_side_effects=True),
+        compiler_params=pltpu.CompilerParams(
+            collective_id=0, has_side_effects=True, vmem_limit_bytes=VMEM_BYTES
+        ),
         name="attend_exchange",
     )(query_rows, key_rows, value_rows, positions.reshape(1, tokens))
-    depth, breadth = cols.shape
+    breadth = cols.shape[1]
     tile = min(TILE, breadth)
+    slots = min(SLOTS, breadth // tile)
     attended, hessian = pl.pallas_call(
         hessian_kernel,
-        grid=(breadth // tile,),
         out_shape=(
             jax.ShapeDtypeStruct((tokens, width), jnp.bfloat16),
             jax.ShapeDtypeStruct((width, breadth), jnp.float32),
         ),
-        in_specs=[
-            pl.BlockSpec((tokens, width), lambda j: (0, 0)),
-            pl.BlockSpec((width, depth), lambda j: (0, 0)),
-            pl.BlockSpec((depth, tile), lambda j: (0, j)),
+        in_specs=[vmem] * 3,
+        out_specs=(pl.BlockSpec(memory_space=pl.ANY), pl.BlockSpec(memory_space=pl.ANY)),
+        scratch_shapes=[
+            pltpu.VMEM((slots, width, tile), jnp.float32),
+            dma,
+            dma((slots,)),
         ],
-        out_specs=(
-            pl.BlockSpec((tokens, width), lambda j: (0, 0)),
-            pl.BlockSpec((width, tile), lambda j: (0, j)),
-        ),
+        compiler_params=pltpu.CompilerParams(vmem_limit_bytes=VMEM_BYTES),
         name="hessian",
     )(own, turned, cols)
     return (attended, hessian)

time: 84.6 us -> 99.3 us (1.17)
  Pallas kernels: 83.7 us -> 94.8 us
  local copies, waits for them, and re-layouts: 0 us -> 3.59 us
    pallas_call x1, Pallas kernels: 67.4 us -> 82.5 us  [on_device(): pl.pallas_call(functools.partial(exchange_kernel, seq_devices, head_devic...]
    pallas_call x1, Pallas kernels: 16.4 us -> 12.3 us  [on_device(): pl.pallas_call(hessian_kernel, out_shape=(jax.ShapeDtypeStruct((tokens, w...]
    unnamed x0 -> x8, local copies, waits for them, and re-layouts: none -> 3.59 us
where the time goes in v1:
time: 99.3 us; the launch traced here: 99 us
  Pallas kernels  94.8 us (95%)
  local copies, waits for them, and re-layouts  3.59 us (4%)
    pallas_call x1, Pallas kernels, on_device(): pl.pallas_call(functools.partial(exchange_kernel, seq_devices, head_devic...  82.5 us
    pallas_call x1, Pallas kernels, on_device(): pl.pallas_call(hessian_kernel, out_shape=(jax.ShapeDtypeStruct((tokens, w...  12.3 us
    unnamed x8, local copies, waits for them, and re-layouts  3.59 us

profile of v1, /device:TPU:25, one launch (start us, length us, event | category | flops | bytes accessed | tf_op | source)
XLA Modules:
  0.0 99.0 jit_solution(11030196294366164157)
XLA Ops:
  0.6 0.0 copy-start
  0.6 1.0 %copy-done = bf16[128,2048]{1,0:T(8,128)(2,1)S(1)} copy-done((bf16[128,2048]{1,0:T(8,128)(2,1)S(1)}, bf16[128,2048]{1,0:T(8,128)(2,1)}, u32[]{:S(2)}) %copy-start) | copy-done | bytes 524312
  1.7 0.0 copy-start.1
  1.7 0.9 copy-done.1
  2.6 0.0 copy-start.2
  2.6 0.9 copy-done.2
  3.6 0.0 copy-start.3
  3.6 0.7 copy-done.3
  4.2 82.5 %attend_exchange.1 = (bf16[128,2048]{1,0:T(8,128)(2,1)S(1)}, bf16[2048,512]{1,0:T(8,128)(2,1)S(1)}, bf16[512,4096]{1,0:T(8,128)(2,1)S(1)}) custom-call(bf16[128,2048]{1,0:T(8,128)(2,1)S(1)} %copy-done, bf16[128,1024]{1,0:T(8,128)(2,1)S(1)} %copy-done.1, bf16[128,1024]{1,0:T(8,128)(2,1)S(1)} %copy-done.2, s32[1,128]{1,0:T(1,128)S(1)} %bitcast.1), custom_call_target="tpu_custom_call" | custom-call | tf_op jit(solution)/shard_map/attend_exchange/pallas_call | solution.py:369
  86.8 12.3 %hessian.1 = (bf16[128,2048]{1,0:T(8,128)(2,1)}, f32[2048,4096]{1,0:T(8,128)}) custom-call(bf16[128,2048]{1,0:T(8,128)(2,1)S(1)} %get-tuple-element.5.own_ref, bf16[2048,512]{1,0:T(8,128)(2,1)S(1)} %get-tuple-element.6.turned_ref, bf16[512,4096]{1,0:T(8,128)(2,1)S(1)} %get-tuple-element.7.cols_ref), custom_call_target="tpu_custom_call" | custom-call | tf_op jit(solution)/shard_map/hessian/pallas_call | solution.py:400
Async XLA Ops:
  0.6 1.0 %copy-start = (bf16[128,2048]{1,0:T(8,128)(2,1)S(1)}, bf16[128,2048]{1,0:T(8,128)(2,1)}, u32[]{:S(2)}) copy-start(bf16[128,2048]{1,0:T(8,128)(2,1)} %q_ref.1) | copy-start | bytes 1572868
  1.7 0.9 copy-start.1
  2.6 0.9 copy-start.2
  3.6 0.7 copy-start.3

commit v2 on v1

--- a/solution.py
+++ b/solution.py
@@ -13,24 +13,28 @@
 SPANS = 4
 CHUNK_HEADS = 2
 TREE_PARTS = 2
-LAG = 2
+LEAD = 0
+LAG = 3
+RAW_PARTS = 0
 TILE = 512
+PIECES = 4
 SLOTS = 4
 VMEM_BYTES = 28 * 1024 * 1024
 MESH = pl.DeviceIdType.MESH
 
 
 def exchange_kernel(
-    seq_devices, head_devices, chunks,
-    q_ref, k_ref, v_ref, pos_ref, attended_ref, turned_ref, cols_ref,
-    rows_ref, kbuf, vbuf, pbuf,
-    kv_send, kv_recv, line_send, line_recv, tree_send, tree_recv, lane_send, lane_recv,
+    seq_devices, head_devices, chunks, raw_parts,
+    q_hbm, k_hbm, v_hbm, pos_hbm, attended_ref, turned_ref, cols_ref,
+    q_ref, raw_ref, rows_ref, kbuf, vbuf, pbuf,
+    load_sems, kv_send, kv_recv, line_send, line_recv, tree_send, tree_recv, lane_send, lane_recv,
 ):
     tokens, width = q_ref.shape
     lanes = head_devices // seq_devices
     bits = seq_devices.bit_length() - 1
     chunk_width = width // chunks
     chunk_heads = chunk_width // HD
+    raw_width = raw_parts * chunk_width
     score_scale = HD ** (-0.5)
     head = lax.axis_index("head")
     span = lax.axis_index("seq")
@@ -53,6 +57,24 @@
 
     def mate(step):
         return node * lanes + (lane + step) % lanes
+
+    key_head = head * (width // HD) // (HEADS // KVH)
+    key_columns = pl.ds(pl.multiple_of(key_head * HD, HD), HD)
+    own_rows = pl.ds(pl.multiple_of(span * tokens, tokens), tokens)
+    loads = [
+        pltpu.make_async_copy(k_hbm.at[:, key_columns], kbuf.at[place], load_sems.at[0]),
+        pltpu.make_async_copy(v_hbm.at[:, key_columns], vbuf.at[place], load_sems.at[1]),
+        pltpu.make_async_copy(pos_hbm, pbuf.at[place], load_sems.at[2]),
+        pltpu.make_async_copy(q_hbm, q_ref, load_sems.at[3]),
+    ]
+    if raw_parts:
+        loads.append(
+            pltpu.make_async_copy(
+                q_hbm.at[:, pl.ds(0, raw_width)], raw_ref.at[own_rows], load_sems.at[4]
+            )
+        )
+    for load in loads:
+        load.start()
 
     barrier = pltpu.get_barrier_semaphore()
     count = 0
@@ -82,16 +104,16 @@
         def _():
             pl.semaphore_wait(barrier, 1)
 
+    for load in loads:
+        load.wait()
     pl.semaphore_wait(barrier, count)
-    key_head = head * (width // HD) // (HEADS // KVH)
-    key_columns = pl.ds(pl.multiple_of(key_head * HD, HD), HD)
 
     def kv_copies(step):
         copies = []
         for which, (src, dst) in enumerate((
-            (k_ref.at[:, key_columns], kbuf.at[place]),
-            (v_ref.at[:, key_columns], vbuf.at[place]),
-            (pos_ref, pbuf.at[place]),
+            (kbuf.at[place], kbuf.at[place]),
+            (vbuf.at[place], vbuf.at[place]),
+            (pbuf.at[place], pbuf.at[place]),
         )):
             copies.append(pltpu.make_async_remote_copy(
                 src_ref=src, dst_ref=dst,
@@ -104,9 +126,9 @@
         source = (place + SPANS - step) % SPANS
         copies = []
         for which, (src, dst) in enumerate((
-            (k_ref.at[:, key_columns], kbuf.at[source]),
-            (v_ref.at[:, key_columns], vbuf.at[source]),
-            (pos_ref, pbuf.at[source]),
+            (kbuf.at[source], kbuf.at[source]),
+            (vbuf.at[source], vbuf.at[source]),
+            (pbuf.at[source], pbuf.at[source]),
         )):
             copies.append(pltpu.make_async_remote_copy(
                 src_ref=src, dst_ref=dst,
@@ -118,9 +140,6 @@
     for step in range(1, SPANS):
         for copy in kv_copies(step):
             copy.start()
-    kbuf[place] = k_ref[:, key_columns]
-    vbuf[place] = v_ref[:, key_columns]
-    pbuf[place] = pos_ref[...]
 
     def row_chunk(block, part):
         return (
@@ -134,8 +153,8 @@
             pl.ds(pl.multiple_of(of_lane * width + part * chunk_width, chunk_width), chunk_width),
         )
 
-    def line_copy(way, block, part):
-        where = rows_ref.at[row_chunk(block, part)]
+    def line_copy(way, block, part, held=rows_ref):
+        where = held.at[row_chunk(block, part)]
         return pltpu.make_async_remote_copy(
             src_ref=where, dst_ref=where,
             send_sem=line_send.at[way, block, part], recv_sem=line_recv.at[block, part],
@@ -156,6 +175,14 @@
             recv_sem=lane_recv.at[step - 1, block, part],
             device_id={"head": mate(step)}, device_id_type=MESH,
         )
+
+    farthest = jnp.maximum(span, seq_devices - 1 - span)
+
+    def walks(block, part):
+        final = jnp.logical_and(
+            jnp.abs(block - span) == farthest, part >= chunks - TREE_PARTS
+        )
+        return jnp.where(final, 0, 1)
 
     def sends(bit, block, part):
         turn = (block + part) % 2
@@ -166,8 +193,8 @@
             middle = 1 - last * (1 - first)
             starts = turn if bit == 1 else 1 - turn
             walk = starts * corner + (1 - starts) * middle
-            early = jnp.where(part < chunks - TREE_PARTS, 1, 0)
-            count = early * walk + (1 - early) * count
+            walked = walks(block, part)
+            count = walked * walk + (1 - walked) * count
         return count == 0
 
     def spread(block, part, source):
@@ -178,15 +205,16 @@
         for step in range(1, lanes):
             lane_copy(step, lane, block, part, source).start()
 
-    def on_row(block, part, up, down):
+    def pass_on(block, part, up, down, held=rows_ref):
         @pl.when(up)
         def _():
-            line_copy(0, block, part).start()
+            line_copy(0, block, part, held).start()
 
         @pl.when(down)
         def _():
-            line_copy(1, block, part).start()
-
+            line_copy(1, block, part, held).start()
+
+    def on_row(block, part):
         @pl.when(root)
         def _():
             spread(block, part, rows_ref.at[row_chunk(block, part)])
@@ -200,6 +228,9 @@
     has_up = span < seq_devices - 1
     has_down = span > 0
 
+    for part in range(raw_parts):
+        pass_on(span, part, has_up, has_down, raw_ref)
+
     for step in range(1, SPANS):
         for copy in kv_arrivals(step):
             copy.wait_recv()
@@ -207,16 +238,16 @@
     keys = kbuf[...].reshape(SPANS * tokens, HD)
     values = vbuf[...].reshape(SPANS * tokens, HD)
     key_places = jnp.concatenate([pbuf[j] for j in range(SPANS)], axis=1)
-    query_places = jnp.broadcast_to(pos_ref[0:1, 0:1], (tokens, 1)) + lax.broadcasted_iota(
-        jnp.int32, (tokens, 1), 0
-    )
-    visible = key_places <= query_places
-
-    def compute(part, carry):
+
+    def attend(held, rows, part, at):
+        query_places = jnp.broadcast_to(pbuf[at][0:1, 0:1], (tokens, 1)) + lax.broadcasted_iota(
+            jnp.int32, (tokens, 1), 0
+        )
+        visible = key_places <= query_places
         pieces = []
         for h in range(chunk_heads):
             columns = pl.ds(pl.multiple_of(part * chunk_width + h * HD, HD), HD)
-            queries = q_ref[:, columns]
+            queries = held[rows, columns]
             scores = lax.dot_general(
                 queries, keys, (((1,), (1,)), ((), ())), preferred_element_type=jnp.float32
             ) * score_scale
@@ -228,24 +259,54 @@
                 weights.astype(jnp.bfloat16), values, preferred_element_type=jnp.float32
             )
             pieces.append((mixed / weight_sum).astype(jnp.bfloat16))
-        joined = jnp.concatenate(pieces, axis=1)
+        return jnp.concatenate(pieces, axis=1)
+
+    def compute(step, carry):
+        part = (step + raw_parts) % chunks
+        joined = attend(q_ref, pl.ds(0, tokens), part, place)
         rows_ref[row_chunk(span, part)] = joined
         attended_ref[:, pl.ds(pl.multiple_of(part * chunk_width, chunk_width), chunk_width)] = joined
-
-        on_row(span, part, has_up, has_down)
+        sent = part >= raw_parts
+        pass_on(span, part, jnp.logical_and(has_up, sent), jnp.logical_and(has_down, sent))
+        on_row(span, part)
         return carry
 
     lax.fori_loop(0, chunks, compute, 0)
 
+    def arrive(way, block, part):
+        up = has_up if way == 0 else False
+        down = has_down if way == 1 else False
+
+        def ready():
+            line_copy(way, block, part).wait_recv()
+            pass_on(block, part, up, down)
+
+        if raw_parts:
+            @pl.when(part >= raw_parts)
+            def _():
+                ready()
+
+            @pl.when(part < raw_parts)
+            def _():
+                line_copy(way, block, part, raw_ref).wait_recv()
+                pass_on(block, part, up, down, raw_ref)
+                rows_ref[row_chunk(block, part)] = attend(
+                    raw_ref, pl.ds(pl.multiple_of(block * tokens, tokens), tokens), part,
+                    block % SPANS,
+                )
+        else:
+            ready()
+        on_row(block, part)
+
+    classes = [(0, False), (1, False)]
+    deepest = bits
     if bits == 2:
+        classes = [(0, True), (1, True)] + classes
+        deepest = 3
         depths = [
             far[turn] * (1 + far[1 - turn]) + 3 * (1 - far[turn]) * far[1 - turn]
             for turn in range(2)
         ]
-        deepest = 3
-    else:
-        depths = [above[0], above[0]]
-        deepest = bits
 
     def relay(item, carry):
         reach, part = item // chunks, item % chunks
@@ -253,20 +314,22 @@
 
         @pl.when(jnp.logical_and(inside, reach <= span))
         def _():
-            block = span - reach
-            line_copy(0, block, part).wait_recv()
-            on_row(block, part, has_up, False)
+            arrive(0, span - reach, part)
 
         @pl.when(jnp.logical_and(inside, span + reach < seq_devices))
         def _():
-            block = span + reach
-            line_copy(1, block, part).wait_recv()
-            on_row(block, part, False, has_down)
-
-        for turn in range(2):
-            late = item - LAG * depths[turn]
+            arrive(1, span + reach, part)
+
+        for turn, walked in classes:
+            late = item - LEAD - LAG * (depths[turn] if walked else above[0])
             distance, piece = late // chunks, late % chunks
             known = jnp.logical_and(not_root, late >= 0)
+
+            def mine(block, piece=piece, turn=turn, walked=walked):
+                match = (block + seq_devices + piece + turn) % 2 == 0
+                if bits == 2:
+                    match = jnp.logical_and(match, walks(block, piece) == (1 if walked else 0))
+                return match
 
             def from_parent(block, piece=piece):
                 source = cols_ref.at[col_chunk(lane, block, piece)]
@@ -275,8 +338,7 @@
 
             @pl.when(
                 jnp.logical_and(
-                    jnp.logical_and(known, distance <= span),
-                    (span + seq_devices - distance + piece + turn) % 2 == 0,
+                    jnp.logical_and(known, distance <= span), mine(span - distance)
                 )
             )
             def _():
@@ -285,10 +347,7 @@
             @pl.when(
                 jnp.logical_and(
                     jnp.logical_and(known, distance > 0),
-                    jnp.logical_and(
-                        span + distance < seq_devices,
-                        (span + distance + piece + turn) % 2 == 0,
-                    ),
+                    jnp.logical_and(span + distance < seq_devices, mine(span + distance)),
                 )
             )
             def _():
@@ -296,7 +355,7 @@
 
         return carry
 
-    lax.fori_loop(0, seq_devices * chunks + LAG * deepest, relay, 0)
+    lax.fori_loop(0, seq_devices * chunks + LEAD + LAG * deepest, relay, 0)
 
     def drain(item, carry):
         block, part = item // chunks, item % chunks
@@ -336,24 +395,34 @@
     def columns(j):
         return pl.ds(pl.multiple_of(j * tile, tile), tile)
 
-    def put(j):
+    rows = out_ref.shape[0] // PIECES
+
+    def put(j, piece):
         slot = j % slots
-        return pltpu.make_async_copy(ring.at[slot], out_ref.at[:, columns(j)], ring_sem.at[slot])
+        where = pl.ds(piece * rows, rows)
+        return pltpu.make_async_copy(
+            ring.at[slot, where], out_ref.at[where, columns(j)], ring_sem.at[slot, piece]
+        )
 
     def body(j, carry):
         @pl.when(j >= slots)
         def _():
-            put(j - slots).wait()
-
-        ring[j % slots] = jnp.dot(
-            turned_ref[...], cols_ref[:, columns(j)], preferred_element_type=jnp.float32
-        )
-        put(j).start()
+            for piece in range(PIECES):
+                put(j - slots, piece).wait()
+
+        block = cols_ref[:, columns(j)]
+        for piece in range(PIECES):
+            where = pl.ds(piece * rows, rows)
+            ring[j % slots, where] = jnp.dot(
+                turned_ref[where, :], block, preferred_element_type=jnp.float32
+            )
+            put(j, piece).start()
         return carry
 
     lax.fori_loop(0, tiles, body, 0)
     for j in range(max(0, tiles - slots), tiles):
-        put(j).wait()
+        for piece in range(PIECES):
+            put(j, piece).wait()
     own.wait()
 
 
@@ -364,22 +433,32 @@
     lanes = head_devices // seq_devices
     bits = seq_devices.bit_length() - 1
     chunks = max(1, width // (CHUNK_HEADS * HD))
+    raw_parts = min(RAW_PARTS, chunks - 1) if seq_devices == SPANS else 0
     vmem = pl.BlockSpec(memory_space=pltpu.VMEM)
+    arguments = [
+        pltpu.with_memory_space_constraint(array, pltpu.HBM)
+        for array in (query_rows, key_rows, value_rows, positions.reshape(1, tokens))
+    ]
     dma = pltpu.SemaphoreType.DMA
     own, turned, cols = pl.pallas_call(
-        functools.partial(exchange_kernel, seq_devices, head_devices, chunks),
+        functools.partial(exchange_kernel, seq_devices, head_devices, chunks, raw_parts),
         out_shape=(
             jax.ShapeDtypeStruct((tokens, width), jnp.bfloat16),
             jax.ShapeDtypeStruct((width, seq_devices * tokens), jnp.bfloat16),
             jax.ShapeDtypeStruct((seq_devices * tokens, lanes * width), jnp.bfloat16),
         ),
-        in_specs=[vmem] * 4,
+        in_specs=[pl.BlockSpec(memory_space=pltpu.HBM)] * 4,
         out_specs=(vmem, vmem, vmem),
         scratch_shapes=[
+            pltpu.VMEM((tokens, width), jnp.bfloat16),
+            pltpu.VMEM(
+                (seq_devices * tokens, max(1, raw_parts) * width // chunks), jnp.bfloat16
+            ),
             pltpu.VMEM((seq_devices * tokens, width), jnp.bfloat16),
             pltpu.VMEM((SPANS, tokens, HD), jnp.bfloat16),
             pltpu.VMEM((SPANS, tokens, HD), jnp.bfloat16),
             pltpu.VMEM((SPANS, 1, tokens), jnp.int32),
+            dma((5,)),
             dma((3, SPANS - 1)),
             dma((3, SPANS - 1)),
             dma((2, seq_devices, chunks)),
@@ -393,7 +472,7 @@
             collective_id=0, has_side_effects=True, vmem_limit_bytes=VMEM_BYTES
         ),
         name="attend_exchange",
-    )(query_rows, key_rows, value_rows, positions.reshape(1, tokens))
+    )(*arguments)
     breadth = cols.shape[1]
     tile = min(TILE, breadth)
     slots = min(SLOTS, breadth // tile)
@@ -408,7 +487,7 @@
         scratch_shapes=[
             pltpu.VMEM((slots, width, tile), jnp.float32),
             dma,
-            dma((slots,)),
+            dma((slots, PIECES)),
         ],
         compiler_params=pltpu.CompilerParams(vmem_limit_bytes=VMEM_BYTES),
         name="hessian",

time: 99.3 us -> 70.2 us (0.71)
  the two profiles are of different devices: /device:TPU:25 before, /device:TPU:3 now
where the time goes in v2:
time: 70.2 us; the launch traced here: 70 us
  Pallas kernels  69.4 us (99%)
    pallas_call x1, Pallas kernels, on_device(): pl.pallas_call(functools.partial(exchange_kernel, seq_devices, head_devic...  57.9 us
    pallas_call x1, Pallas kernels, on_device(): pl.pallas_call(hessian_kernel, out_shape=(jax.ShapeDtypeStruct((tokens, w...  11.5 us

profile of v2, /device:TPU:3, one launch (start us, length us, event | category | flops | bytes accessed | tf_op | source)
XLA Modules:
  0.0 70.0 jit_solution(14589089147923146251)
XLA Ops:
  0.6 57.9 %attend_exchange.1 = (bf16[128,2048]{1,0:T(8,128)(2,1)S(1)}, bf16[2048,512]{1,0:T(8,128)(2,1)S(1)}, bf16[512,4096]{1,0:T(8,128)(2,1)S(1)}) custom-call(bf16[128,2048]{1,0:T(8,128)(2,1)} %q_hbm.1, bf16[128,1024]{1,0:T(8,128)(2,1)} %k_hbm.1, bf16[128,1024]{1,0:T(8,128)(2,1)} %v_hbm.1, s32[1,128]{1,0:T(1,128)} %bitcast.1), custom_call_target="tpu_custom_call" | custom-call | tf_op jit(solution)/shard_map/attend_exchange/pallas_call | solution.py:443
  58.5 11.5 %hessian.1 = (bf16[128,2048]{1,0:T(8,128)(2,1)}, f32[2048,4096]{1,0:T(8,128)}) custom-call(bf16[128,2048]{1,0:T(8,128)(2,1)S(1)} %get-tuple-element.5.own_ref, bf16[2048,512]{1,0:T(8,128)(2,1)S(1)} %get-tuple-element.6.turned_ref, bf16[512,4096]{1,0:T(8,128)(2,1)S(1)} %get-tuple-element.7.cols_ref), custom_call_target="tpu_custom_call" | custom-call | tf_op jit(solution)/shard_map/hessian/pallas_call | solution.py:479

commit v3 on v2

--- a/solution.py
+++ b/solution.py
@@ -12,10 +12,12 @@
 HD = 128
 SPANS = 4
 CHUNK_HEADS = 2
-TREE_PARTS = 2
+COMPUTE_HEADS = 4
 LEAD = 0
-LAG = 3
-RAW_PARTS = 0
+LAG_ONE = 2
+LAG_TWO = 3
+LAG_THREE = 5
+RAW_PAIRS = 1
 TILE = 512
 PIECES = 4
 SLOTS = 4
@@ -24,7 +26,7 @@
 
 
 def exchange_kernel(
-    seq_devices, head_devices, chunks, raw_parts,
+    seq_devices, head_devices, chunks, raw_pairs,
     q_hbm, k_hbm, v_hbm, pos_hbm, attended_ref, turned_ref, cols_ref,
     q_ref, raw_ref, rows_ref, kbuf, vbuf, pbuf,
     load_sems, kv_send, kv_recv, line_send, line_recv, tree_send, tree_recv, lane_send, lane_recv,
@@ -34,7 +36,7 @@
     bits = seq_devices.bit_length() - 1
     chunk_width = width // chunks
     chunk_heads = chunk_width // HD
-    raw_width = raw_parts * chunk_width
+    raw_width = raw_pairs * 2 * chunk_width
     score_scale = HD ** (-0.5)
     head = lax.axis_index("head")
     span = lax.axis_index("seq")
@@ -67,7 +69,7 @@
         pltpu.make_async_copy(pos_hbm, pbuf.at[place], load_sems.at[2]),
         pltpu.make_async_copy(q_hbm, q_ref, load_sems.at[3]),
     ]
-    if raw_parts:
+    if raw_pairs:
         loads.append(
             pltpu.make_async_copy(
                 q_hbm.at[:, pl.ds(0, raw_width)], raw_ref.at[own_rows], load_sems.at[4]
@@ -153,58 +155,86 @@
             pl.ds(pl.multiple_of(of_lane * width + part * chunk_width, chunk_width), chunk_width),
         )
 
+    def block_rows(block):
+        return pl.ds(pl.multiple_of(block * tokens, tokens), tokens)
+
     def line_copy(way, block, part, held=rows_ref):
         where = held.at[row_chunk(block, part)]
         return pltpu.make_async_remote_copy(
             src_ref=where, dst_ref=where,
-            send_sem=line_send.at[way, block, part], recv_sem=line_recv.at[block, part],
+            send_sem=line_send.at[way, block], recv_sem=line_recv.at[block, part],
             device_id={"seq": span + 1 - 2 * way}, device_id_type=MESH,
         )
 
-    def tree_copy(bit, block, part, source):
+    def tree_copy(bit, kind, turn, block, part, source):
         return pltpu.make_async_remote_copy(
             src_ref=source, dst_ref=cols_ref.at[col_chunk(lane, block, part)],
-            send_sem=tree_send.at[bit, block, part], recv_sem=tree_recv.at[block, part],
+            send_sem=tree_send.at[bit, kind, turn, block], recv_sem=tree_recv.at[block, part],
             device_id={"head": flip(bit)}, device_id_type=MESH,
         )
 
     def lane_copy(step, of_lane, block, part, source):
         return pltpu.make_async_remote_copy(
             src_ref=source, dst_ref=cols_ref.at[col_chunk(of_lane, block, part)],
-            send_sem=lane_send.at[step - 1, block, part],
-            recv_sem=lane_recv.at[step - 1, block, part],
+            send_sem=lane_send.at[step - 1, block],
+            recv_sem=lane_recv.at[step - 1, block],
             device_id={"head": mate(step)}, device_id_type=MESH,
         )
 
+    pairs = chunks // 2
     farthest = jnp.maximum(span, seq_devices - 1 - span)
-
-    def walks(block, part):
-        final = jnp.logical_and(
-            jnp.abs(block - span) == farthest, part >= chunks - TREE_PARTS
-        )
-        return jnp.where(final, 0, 1)
-
-    def sends(bit, block, part):
-        turn = (block + part) % 2
-        count = turn * above[bit] + (1 - turn) * below[bit]
-        if bits == 2:
-            first, last = far[bit], far[1 - bit]
-            corner = (first - last) * (first - last)
-            middle = 1 - last * (1 - first)
-            starts = turn if bit == 1 else 1 - turn
-            walk = starts * corner + (1 - starts) * middle
-            walked = walks(block, part)
-            count = walked * walk + (1 - walked) * count
-        return count == 0
-
-    def spread(block, part, source):
+    tree_now = [
+        [turn * above[bit] + (1 - turn) * below[bit] == 0 for bit in range(bits)]
+        for turn in range(2)
+    ]
+    tree_depth = above[0]
+    if bits == 2:
+        walk_now = []
+        depths = []
+        for turn in range(2):
+            first, last = far[turn], far[1 - turn]
+            corner = first == last
+            middle = jnp.logical_and(first == 1, last == 0)
+            walk_now.append([corner, middle] if turn == 0 else [middle, corner])
+            depths.append(first * (1 + last) + 3 * (1 - first) * last)
+        lags = [
+            jnp.where(depth == 1, LAG_ONE, jnp.where(depth == 2, LAG_TWO, LAG_THREE))
+            for depth in depths
+        ]
+        tree_lag = jnp.where(tree_depth == 1, LAG_ONE, LAG_TWO)
+        longest = LAG_THREE
+        kinds = 2
+    else:
+        walk_now = tree_now
+        lags = [LAG_ONE * tree_depth] * 2
+        longest = LAG_ONE * bits
+        kinds = 1
+
+    def share(turn, block, part, source, kind):
+        now = tree_now if kind else walk_now
         for bit in range(bits):
-            @pl.when(sends(bit, block, part))
+            @pl.when(now[turn][bit])
             def _():
-                tree_copy(bit, block, part, source).start()
+                tree_copy(bit, kind, turn, block, part, source).start()
         for step in range(1, lanes):
             lane_copy(step, lane, block, part, source).start()
 
+    def spread(turn, block, pair):
+        part = 2 * pair + turn
+        source = rows_ref.at[row_chunk(block, part)]
+        if kinds == 2:
+            final = jnp.abs(block - span) == farthest
+
+            @pl.when(final)
+            def _():
+                share(turn, block, part, source, 1)
+
+            @pl.when(jnp.logical_not(final))
+            def _():
+                share(turn, block, part, source, 0)
+        else:
+            share(turn, block, part, source, 0)
+
     def pass_on(block, part, up, down, held=rows_ref):
         @pl.when(up)
         def _():
@@ -214,21 +244,24 @@
         def _():
             line_copy(1, block, part, held).start()
 
-    def on_row(block, part):
+    def pair_columns(pair, base=0):
+        return pl.ds(pl.multiple_of(base + pair * 2 * chunk_width, 2 * chunk_width), 2 * chunk_width)
+
+    def on_rows(block, pair):
+        rows = block_rows(block)
+
         @pl.when(root)
         def _():
-            spread(block, part, rows_ref.at[row_chunk(block, part)])
-            cols_ref[col_chunk(lane, block, part)] = rows_ref[row_chunk(block, part)]
-
-        turned_ref[
-            pl.ds(pl.multiple_of(part * chunk_width, chunk_width), chunk_width),
-            pl.ds(pl.multiple_of(block * tokens, tokens), tokens),
-        ] = rows_ref[row_chunk(block, part)].T
+            for turn in range(2):
+                spread(turn, block, pair)
+            cols_ref[rows, pair_columns(pair, lane * width)] = rows_ref[rows, pair_columns(pair)]
+
+        turned_ref[pair_columns(pair), rows] = rows_ref[rows, pair_columns(pair)].T
 
     has_up = span < seq_devices - 1
     has_down = span > 0
 
-    for part in range(raw_parts):
+    for part in range(2 * raw_pairs):
         pass_on(span, part, has_up, has_down, raw_ref)
 
     for step in range(1, SPANS):
@@ -239,15 +272,14 @@
     values = vbuf[...].reshape(SPANS * tokens, HD)
     key_places = jnp.concatenate([pbuf[j] for j in range(SPANS)], axis=1)
 
-    def attend(held, rows, part, at):
+    def attend(held, rows, start, heads, at):
         query_places = jnp.broadcast_to(pbuf[at][0:1, 0:1], (tokens, 1)) + lax.broadcasted_iota(
             jnp.int32, (tokens, 1), 0
         )
         visible = key_places <= query_places
         pieces = []
-        for h in range(chunk_heads):
-            columns = pl.ds(pl.multiple_of(part * chunk_width + h * HD, HD), HD)
-            queries = held[rows, columns]
+        for h in range(heads):
+            queries = held[rows, pl.ds(pl.multiple_of(start + h * HD, HD), HD)]
             scores = lax.dot_general(
                 queries, keys, (((1,), (1,)), ((), ())), preferred_element_type=jnp.float32
             ) * score_scale
@@ -261,124 +293,169 @@
             pieces.append((mixed / weight_sum).astype(jnp.bfloat16))
         return jnp.concatenate(pieces, axis=1)
 
+    batch = max(1, min(COMPUTE_HEADS // (2 * chunk_heads), pairs - raw_pairs))
+    while pairs % batch or raw_pairs % batch:
+        batch -= 1
+
     def compute(step, carry):
-        part = (step + raw_parts) % chunks
-        joined = attend(q_ref, pl.ds(0, tokens), part, place)
-        rows_ref[row_chunk(span, part)] = joined
-        attended_ref[:, pl.ds(pl.multiple_of(part * chunk_width, chunk_width), chunk_width)] = joined
-        sent = part >= raw_parts
-        pass_on(span, part, jnp.logical_and(has_up, sent), jnp.logical_and(has_down, sent))
-        on_row(span, part)
+        raw_steps = raw_pairs // batch
+        steps = pairs // batch
+        where = step + raw_steps
+        group = jnp.where(where >= steps, where - steps, where)
+        start = group * (batch * 2 * chunk_width)
+        joined = attend(q_ref, pl.ds(0, tokens), start, batch * 2 * chunk_heads, place)
+        columns = pl.ds(pl.multiple_of(start, batch * 2 * chunk_width), batch * 2 * chunk_width)
+        rows_ref[own_rows, columns] = joined
+        attended_ref[:, columns] = joined
+        sent = group >= raw_steps
+        for which in range(batch):
+            for turn in range(2):
+                pass_on(
+                    span, 2 * (group * batch + which) + turn,
+                    jnp.logical_and(has_up, sent), jnp.logical_and(has_down, sent),
+                )
+        for which in range(batch):
+            on_rows(span, group * batch + which)
         return carry
 
-    lax.fori_loop(0, chunks, compute, 0)
-
-    def arrive(way, block, part):
+    lax.fori_loop(0, pairs // batch, compute, 0)
+
+    def arrive(way, block, pair):
         up = has_up if way == 0 else False
         down = has_down if way == 1 else False
 
-        def ready():
-            line_copy(way, block, part).wait_recv()
-            pass_on(block, part, up, down)
-
-        if raw_parts:
-            @pl.when(part >= raw_parts)
+        def ready(held):
+            for turn in range(2):
+                line_copy(way, block, 2 * pair + turn, held).wait_recv()
+                pass_on(block, 2 * pair + turn, up, down, held)
+
+        if raw_pairs:
+            @pl.when(pair >= raw_pairs)
             def _():
-                ready()
-
-            @pl.when(part < raw_parts)
+                ready(rows_ref)
+
+            @pl.when(pair < raw_pairs)
             def _():
-                line_copy(way, block, part, raw_ref).wait_recv()
-                pass_on(block, part, up, down, raw_ref)
-                rows_ref[row_chunk(block, part)] = attend(
-                    raw_ref, pl.ds(pl.multiple_of(block * tokens, tokens), tokens), part,
-                    block % SPANS,
+                ready(raw_ref)
+                rows = block_rows(block)
+                rows_ref[rows, pair_columns(pair)] = attend(
+                    raw_ref, rows, pair * 2 * chunk_width, 2 * chunk_heads, lax.rem(block, SPANS)
                 )
         else:
-            ready()
-        on_row(block, part)
-
-    classes = [(0, False), (1, False)]
-    deepest = bits
-    if bits == 2:
-        classes = [(0, True), (1, True)] + classes
-        deepest = 3
-        depths = [
-            far[turn] * (1 + far[1 - turn]) + 3 * (1 - far[turn]) * far[1 - turn]
-            for turn in range(2)
-        ]
+            ready(rows_ref)
+        on_rows(block, pair)
+
+    def from_parent(turn, block, pair, kind):
+        part = 2 * pair + turn
+        source = cols_ref.at[col_chunk(lane, block, part)]
+        tree_copy(0, kind, turn, block, part, source).wait_recv()
+        share(turn, block, part, source, kind)
+
+    def at_distance(distance, known, act):
+        @pl.when(jnp.logical_and(known, distance <= span))
+        def _():
+            act(span - distance)
+
+        @pl.when(
+            jnp.logical_and(known, jnp.logical_and(distance > 0, span + distance < seq_devices))
+        )
+        def _():
+            act(span + distance)
+
+    def behind(item, lag):
+        late = item - LEAD - lag
+        distance = lax.div(jnp.maximum(late, 0), pairs)
+        pair = jnp.maximum(late, 0) - distance * pairs
+        if raw_pairs:
+            turned = jnp.where(pair < pairs - raw_pairs, pair + raw_pairs, pair + raw_pairs - pairs)
+            pair = jnp.where(distance == 0, turned, pair)
+        return distance, pair, jnp.logical_and(not_root, late >= 0)
+
+    def walk(item):
+        for turn in range(2):
+            distance, pair, known = behind(item, lags[turn])
+            if kinds == 2:
+                known = jnp.logical_and(known, distance != farthest)
+            at_distance(distance, known, lambda block: from_parent(turn, block, pair, 0))
+        if kinds == 2:
+            distance, pair, known = behind(item, tree_lag)
+
+            def both(block):
+                for turn in range(2):
+                    from_parent(turn, block, pair, 1)
+
+            at_distance(distance, jnp.logical_and(known, distance == farthest), both)
 
     def relay(item, carry):
-        reach, part = item // chunks, item % chunks
-        inside = jnp.logical_and(reach > 0, reach < seq_devices)
-
-        @pl.when(jnp.logical_and(inside, reach <= span))
-        def _():
-            arrive(0, span - reach, part)
-
-        @pl.when(jnp.logical_and(inside, span + reach < seq_devices))
-        def _():
-            arrive(1, span + reach, part)
-
-        for turn, walked in classes:
-            late = item - LEAD - LAG * (depths[turn] if walked else above[0])
-            distance, piece = late // chunks, late % chunks
-            known = jnp.logical_and(not_root, late >= 0)
-
-            def mine(block, piece=piece, turn=turn, walked=walked):
-                match = (block + seq_devices + piece + turn) % 2 == 0
-                if bits == 2:
-                    match = jnp.logical_and(match, walks(block, piece) == (1 if walked else 0))
-                return match
-
-            def from_parent(block, piece=piece):
-                source = cols_ref.at[col_chunk(lane, block, piece)]
-                tree_copy(0, block, piece, source).wait_recv()
-                spread(block, piece, source)
-
-            @pl.when(
-                jnp.logical_and(
-                    jnp.logical_and(known, distance <= span), mine(span - distance)
-                )
+        reach = lax.div(item, pairs)
+        pair = item - reach * pairs
+
+        @pl.when(reach <= span)
+        def _():
+            arrive(0, span - reach, pair)
+
+        @pl.when(span + reach < seq_devices)
+        def _():
+            arrive(1, span + reach, pair)
+
+        walk(item)
+        return carry
+
+    def late_walk(item, carry):
+        walk(item)
+        return carry
+
+    lax.fori_loop(0, pairs, late_walk, 0)
+    lax.fori_loop(pairs, seq_devices * pairs, relay, 0)
+    lax.fori_loop(seq_devices * pairs, seq_devices * pairs + LEAD + longest, late_walk, 0)
+
+    def sized(rows, columns, send, recv):
+        view = rows_ref.at[pl.ds(0, rows), pl.ds(0, columns)]
+        return pltpu.make_async_remote_copy(
+            src_ref=view, dst_ref=view, send_sem=send, recv_sem=recv,
+            device_id={"head": mate(1)}, device_id_type=MESH,
+        )
+
+    def drain(block, carry):
+        spare = tree_recv.at[block, 0]
+
+        @pl.when(jnp.logical_and(has_up, block <= span))
+        def _():
+            sized(tokens, width, line_send.at[0, block], spare).wait_send()
+
+        @pl.when(jnp.logical_and(has_down, block >= span))
+        def _():
+            sized(tokens, width, line_send.at[1, block], spare).wait_send()
+
+        final = jnp.abs(block - span) == farthest
+        for bit in range(bits):
+            for turn in range(2):
+                def wait_tree(kind):
+                    sized(
+                        tokens, pairs * chunk_width, tree_send.at[bit, kind, turn, block], spare
+                    ).wait_send()
+
+                if kinds == 2:
+                    @pl.when(jnp.logical_and(walk_now[turn][bit], jnp.logical_not(final)))
+                    def _():
+                        wait_tree(0)
+
+                    @pl.when(jnp.logical_and(tree_now[turn][bit], final))
+                    def _():
+                        wait_tree(1)
+                else:
+                    @pl.when(walk_now[turn][bit])
+                    def _():
+                        wait_tree(0)
+        for step in range(1, lanes):
+            whole = sized(
+                tokens, width, lane_send.at[step - 1, block], lane_recv.at[step - 1, block]
             )
-            def _():
-                from_parent(span - distance)
-
-            @pl.when(
-                jnp.logical_and(
-                    jnp.logical_and(known, distance > 0),
-                    jnp.logical_and(span + distance < seq_devices, mine(span + distance)),
-                )
-            )
-            def _():
-                from_parent(span + distance)
-
+            whole.wait_send()
+            whole.wait_recv()
         return carry
 
-    lax.fori_loop(0, seq_devices * chunks + LEAD + LAG * deepest, relay, 0)
-
-    def drain(item, carry):
-        block, part = item // chunks, item % chunks
-        source = cols_ref.at[col_chunk(lane, block, part)]
-
-        @pl.when(jnp.logical_and(has_up, block <= span))
-        def _():
-            line_copy(0, block, part).wait_send()
-
-        @pl.when(jnp.logical_and(has_down, block >= span))
-        def _():
-            line_copy(1, block, part).wait_send()
-
-        for bit in range(bits):
-            @pl.when(sends(bit, block, part))
-            def _():
-                tree_copy(bit, block, part, source).wait_send()
-        for step in range(1, lanes):
-            lane_copy(step, lane, block, part, source).wait_send()
-            lane_copy(step, (lane + lanes - step) % lanes, block, part, source).wait_recv()
-        return carry
-
-    lax.fori_loop(0, seq_devices * chunks, drain, 0)
+    lax.fori_loop(0, seq_devices, drain, 0)
 
     for step in range(1, SPANS):
         for copy in kv_copies(step):
@@ -432,8 +509,8 @@
     head_devices = lax.axis_size("head")
     lanes = head_devices // seq_devices
     bits = seq_devices.bit_length() - 1
-    chunks = max(1, width // (CHUNK_HEADS * HD))
-    raw_parts = min(RAW_PARTS, chunks - 1) if seq_devices == SPANS else 0
+    chunks = max(2, width // (CHUNK_HEADS * HD))
+    raw_pairs = min(RAW_PAIRS, chunks // 2 - 1) if seq_devices == SPANS else 0
     vmem = pl.BlockSpec(memory_space=pltpu.VMEM)
     arguments = [
         pltpu.with_memory_space_constraint(array, pltpu.HBM)
@@ -441,7 +518,7 @@
     ]
     dma = pltpu.SemaphoreType.DMA
     own, turned, cols = pl.pallas_call(
-        functools.partial(exchange_kernel, seq_devices, head_devices, chunks, raw_parts),
+        functools.partial(exchange_kernel, seq_devices, head_devices, chunks, raw_pairs),
         out_shape=(
             jax.ShapeDtypeStruct((tokens, width), jnp.bfloat16),
             jax.ShapeDtypeStruct((width, seq_devices * tokens), jnp.bfloat16),
@@ -452,7 +529,7 @@
         scratch_shapes=[
             pltpu.VMEM((tokens, width), jnp.bfloat16),
             pltpu.VMEM(
-                (seq_devices * tokens, max(1, raw_parts) * width // chunks), jnp.bfloat16
+                (seq_devices * tokens, max(1, 2 * raw_pairs) * width // chunks), jnp.bfloat16
             ),
             pltpu.VMEM((seq_devices * tokens, width), jnp.bfloat16),
             pltpu.VMEM((SPANS, tokens, HD), jnp.bfloat16),
@@ -461,12 +538,12 @@
             dma((5,)),
             dma((3, SPANS - 1)),
             dma((3, SPANS - 1)),
-            dma((2, seq_devices, chunks)),
+            dma((2, seq_devices)),
             dma((seq_devices, chunks)),
-            dma((bits, seq_devices, chunks)),
+            dma((bits, 2 if bits == 2 else 1, 2, seq_devices)),
             dma((seq_devices, chunks)),
-            dma((lanes - 1, seq_devices, chunks)),
-            dma((lanes - 1, seq_devices, chunks)),
+            dma((lanes - 1, seq_devices)),
+            dma((lanes - 1, seq_devices)),
         ],
         compiler_params=pltpu.CompilerParams(
             collective_id=0, has_side_effects=True, vmem_limit_bytes=VMEM_BYTES

time: 70.2 us -> 66.5 us (0.947)
  the two profiles are of different devices: /device:TPU:3 before, /device:TPU:25 now
where the time goes in v3:
time: 66.5 us; the launch traced here: 65.4 us
  Pallas kernels  64.8 us (97%)
    pallas_call x1, Pallas kernels, on_device(): pl.pallas_call(functools.partial(exchange_kernel, seq_devices, head_devic...  53.3 us
    pallas_call x1, Pallas kernels, on_device(): pl.pallas_call(hessian_kernel, out_shape=(jax.ShapeDtypeStruct((tokens, w...  11.5 us

profile of v3, /device:TPU:25, one launch (start us, length us, event | category | flops | bytes accessed | tf_op | source)
XLA Modules:
  0.0 65.4 jit_solution(4026367296963496652)
XLA Ops:
  0.6 53.3 %attend_exchange.1 = (bf16[128,2048]{1,0:T(8,128)(2,1)S(1)}, bf16[2048,512]{1,0:T(8,128)(2,1)S(1)}, bf16[512,4096]{1,0:T(8,128)(2,1)S(1)}) custom-call(bf16[128,2048]{1,0:T(8,128)(2,1)} %q_hbm.1, bf16[128,1024]{1,0:T(8,128)(2,1)} %k_hbm.1, bf16[128,1024]{1,0:T(8,128)(2,1)} %v_hbm.1, s32[1,128]{1,0:T(1,128)} %bitcast.1), custom_call_target="tpu_custom_call" | custom-call | tf_op jit(solution)/shard_map/attend_exchange/pallas_call | solution.py:520
  54.0 11.5 %hessian.1 = (bf16[128,2048]{1,0:T(8,128)(2,1)}, f32[2048,4096]{1,0:T(8,128)}) custom-call(bf16[128,2048]{1,0:T(8,128)(2,1)S(1)} %get-tuple-element.5.own_ref, bf16[2048,512]{1,0:T(8,128)(2,1)S(1)} %get-tuple-element.6.turned_ref, bf16[512,4096]{1,0:T(8,128)(2,1)S(1)} %get-tuple-element.7.cols_ref), custom_call_target="tpu_custom_call" | custom-call | tf_op jit(solution)/shard_map/hessian/pallas_call | solution.py:556

commit v4 on v3

--- a/solution.py
+++ b/solution.py
@@ -14,7 +14,8 @@
 CHUNK_HEADS = 2
 COMPUTE_HEADS = 4
 LEAD = 0
-LAG_ONE = 2
+MIDDLE_LEAD = 1
+LAG_ONE = 1
 LAG_TWO = 3
 LAG_THREE = 5
 RAW_PAIRS = 1
@@ -29,7 +30,7 @@
     seq_devices, head_devices, chunks, raw_pairs,
     q_hbm, k_hbm, v_hbm, pos_hbm, attended_ref, turned_ref, cols_ref,
     q_ref, raw_ref, rows_ref, kbuf, vbuf, pbuf,
-    load_sems, kv_send, kv_recv, line_send, line_recv, tree_send, tree_recv, lane_send, lane_recv,
+    load_sems, detour, landed, detour_load, detour_send, detour_recv, onward_send, kv_send, kv_recv, line_send, line_recv, tree_send, tree_recv, lane_send, lane_recv,
 ):
     tokens, width = q_ref.shape
     lanes = head_devices // seq_devices
@@ -56,6 +57,13 @@
 
     def peer(step):
         return group + (place + step) % SPANS
+
+    shifted = bits == 2 and seq_devices == SPANS
+    ends = (0, seq_devices - 1)
+    at_end = jnp.logical_or(span == 0, span == seq_devices - 1)
+
+    def across(move):
+        return head + sum(flip(bit) - head for bit in range(bits) if move // 2**bit % 2)
 
     def mate(step):
         return node * lanes + (lane + step) % lanes
@@ -78,13 +86,62 @@
     for load in loads:
         load.start()
 
+    def end_columns(end):
+        first = (end * lanes + lane) * (width // HD) // (HEADS // KVH)
+        return pl.ds(pl.multiple_of(first * HD, HD), HD)
+
+    def detour_loads(which_end):
+        columns = end_columns(ends[which_end])
+        return [
+            pltpu.make_async_copy(
+                array.at[:, columns], detour.at[which_end, which], detour_load.at[which_end, which]
+            )
+            for which, array in enumerate((k_hbm, v_hbm))
+        ]
+
+    def detour_copies(which_end):
+        return [
+            pltpu.make_async_remote_copy(
+                src_ref=detour.at[which_end, which], dst_ref=landed.at[which],
+                send_sem=detour_send.at[which_end, which], recv_sem=detour_recv.at[which],
+                device_id={"seq": ends[which_end]}, device_id_type=MESH,
+            )
+            for which in range(2)
+        ]
+
+    def onward_copies():
+        hops = lax.rem(span - node + seq_devices - 1, seq_devices)
+        return [
+            pltpu.make_async_remote_copy(
+                src_ref=landed.at[which], dst_ref=buffer.at[node],
+                send_sem=onward_send.at[which], recv_sem=kv_recv.at[which, hops],
+                device_id={"head": span * lanes + lane}, device_id_type=MESH,
+            )
+            for which, buffer in enumerate((kbuf, vbuf))
+        ]
+
+    def each_end(act):
+        for which_end in range(2):
+            @pl.when(jnp.logical_and(root, span != ends[which_end]))
+            def _():
+                act(which_end)
+
+    if shifted:
+        @pl.when(root)
+        def _():
+            for which_end in range(2):
+                for load in detour_loads(which_end):
+                    load.start()
+
     barrier = pltpu.get_barrier_semaphore()
     count = 0
     for step in range(1, SPANS):
         pl.semaphore_signal(barrier, inc=1, device_id={"seq": peer(step)}, device_id_type=MESH)
         count += 1
-    for bit in range(bits):
-        pl.semaphore_signal(barrier, inc=1, device_id={"head": flip(bit)}, device_id_type=MESH)
+    for move in (range(1, 2**bits) if shifted else [2**bit for bit in range(bits)]):
+        pl.semaphore_signal(
+            barrier, inc=1, device_id={"head": across(move)}, device_id_type=MESH
+        )
         count += 1
     for step in range(1, lanes):
         pl.semaphore_signal(barrier, inc=1, device_id={"head": mate(step)}, device_id_type=MESH)
@@ -108,6 +165,13 @@
 
     for load in loads:
         load.wait()
+    if shifted:
+        @pl.when(root)
+        def _():
+            for which_end in range(2):
+                for load in detour_loads(which_end):
+                    load.wait()
+
     pl.semaphore_wait(barrier, count)
 
     def kv_copies(step):
@@ -139,9 +203,31 @@
             ))
         return copies
 
+    def each_kv(step, act):
+        goal = peer(step)
+        copies = kv_copies(step)
+        act(copies[2])
+        if shifted:
+            round_about = jnp.logical_and(
+                node == goal, jnp.logical_or(goal == 0, goal == seq_devices - 1)
+            )
+
+            @pl.when(jnp.logical_not(round_about))
+            def _():
+                act(copies[0])
+                act(copies[1])
+        else:
+            act(copies[0])
+            act(copies[1])
+
     for step in range(1, SPANS):
-        for copy in kv_copies(step):
-            copy.start()
+        each_kv(step, lambda copy: copy.start())
+    if shifted:
+        def depart(which_end):
+            for copy in detour_copies(which_end):
+                copy.start()
+
+        each_end(depart)
 
     def row_chunk(block, part):
         return (
@@ -247,13 +333,16 @@
     def pair_columns(pair, base=0):
         return pl.ds(pl.multiple_of(base + pair * 2 * chunk_width, 2 * chunk_width), 2 * chunk_width)
 
-    def on_rows(block, pair):
+    def on_rows(block, pair, fresh):
         rows = block_rows(block)
 
-        @pl.when(root)
+        @pl.when(jnp.logical_and(root, fresh))
         def _():
             for turn in range(2):
                 spread(turn, block, pair)
+
+        @pl.when(root)
+        def _():
             cols_ref[rows, pair_columns(pair, lane * width)] = rows_ref[rows, pair_columns(pair)]
 
         turned_ref[pair_columns(pair), rows] = rows_ref[rows, pair_columns(pair)].T
@@ -267,6 +356,13 @@
     for step in range(1, SPANS):
         for copy in kv_arrivals(step):
             copy.wait_recv()
+
+    if shifted:
+        @pl.when(jnp.logical_and(at_end, not_root))
+        def _():
+            for arrival, copy in zip(detour_copies(0), onward_copies()):
+                arrival.wait_recv()
+                copy.start()
 
     keys = kbuf[...].reshape(SPANS * tokens, HD)
     values = vbuf[...].reshape(SPANS * tokens, HD)
@@ -315,35 +411,44 @@
                     jnp.logical_and(has_up, sent), jnp.logical_and(has_down, sent),
                 )
         for which in range(batch):
-            on_rows(span, group * batch + which)
+            on_rows(span, group * batch + which, True)
         return carry
 
     lax.fori_loop(0, pairs // batch, compute, 0)
 
-    def arrive(way, block, pair):
+    def forward(way, block, pair):
         up = has_up if way == 0 else False
         down = has_down if way == 1 else False
 
-        def ready(held):
+        def ready(held, final):
             for turn in range(2):
                 line_copy(way, block, 2 * pair + turn, held).wait_recv()
                 pass_on(block, 2 * pair + turn, up, down, held)
+                if final:
+                    @pl.when(root)
+                    def _():
+                        spread(turn, block, pair)
 
         if raw_pairs:
             @pl.when(pair >= raw_pairs)
             def _():
-                ready(rows_ref)
+                ready(rows_ref, True)
 
             @pl.when(pair < raw_pairs)
             def _():
-                ready(raw_ref)
+                ready(raw_ref, False)
+        else:
+            ready(rows_ref, True)
+
+    def settle(block, pair):
+        if raw_pairs:
+            @pl.when(pair < raw_pairs)
+            def _():
                 rows = block_rows(block)
                 rows_ref[rows, pair_columns(pair)] = attend(
                     raw_ref, rows, pair * 2 * chunk_width, 2 * chunk_heads, lax.rem(block, SPANS)
                 )
-        else:
-            ready(rows_ref)
-        on_rows(block, pair)
+        on_rows(block, pair, pair < raw_pairs)
 
     def from_parent(turn, block, pair, kind):
         part = 2 * pair + turn
@@ -363,7 +468,7 @@
             act(span + distance)
 
     def behind(item, lag):
-        late = item - LEAD - lag
+        late = item - jnp.where(at_end, LEAD, MIDDLE_LEAD) - lag
         distance = lax.div(jnp.maximum(late, 0), pairs)
         pair = jnp.maximum(late, 0) - distance * pairs
         if raw_pairs:
@@ -390,13 +495,24 @@
         reach = lax.div(item, pairs)
         pair = item - reach * pairs
 
-        @pl.when(reach <= span)
-        def _():
-            arrive(0, span - reach, pair)
-
-        @pl.when(span + reach < seq_devices)
-        def _():
-            arrive(1, span + reach, pair)
+        from_low = reach <= span
+        from_high = span + reach < seq_devices
+
+        @pl.when(from_low)
+        def _():
+            forward(0, span - reach, pair)
+
+        @pl.when(from_high)
+        def _():
+            forward(1, span + reach, pair)
+
+        @pl.when(from_low)
+        def _():
+            settle(span - reach, pair)
+
+        @pl.when(from_high)
+        def _():
+            settle(span + reach, pair)
 
         walk(item)
         return carry
@@ -407,7 +523,7 @@
 
     lax.fori_loop(0, pairs, late_walk, 0)
     lax.fori_loop(pairs, seq_devices * pairs, relay, 0)
-    lax.fori_loop(seq_devices * pairs, seq_devices * pairs + LEAD + longest, late_walk, 0)
+    lax.fori_loop(seq_devices * pairs, seq_devices * pairs + max(LEAD, MIDDLE_LEAD) + longest, late_walk, 0)
 
     def sized(rows, columns, send, recv):
         view = rows_ref.at[pl.ds(0, rows), pl.ds(0, columns)]
@@ -458,8 +574,18 @@
     lax.fori_loop(0, seq_devices, drain, 0)
 
     for step in range(1, SPANS):
-        for copy in kv_copies(step):
-            copy.wait_send()
+        each_kv(step, lambda copy: copy.wait_send())
+    if shifted:
+        def departed(which_end):
+            for copy in detour_copies(which_end):
+                copy.wait_send()
+
+        each_end(departed)
+
+        @pl.when(jnp.logical_and(at_end, not_root))
+        def _():
+            for copy in onward_copies():
+                copy.wait_send()
 
 
 def hessian_kernel(own_ref, turned_ref, cols_ref, attended_ref, out_ref, ring, own_sem, ring_sem):
@@ -536,6 +662,12 @@
             pltpu.VMEM((SPANS, tokens, HD), jnp.bfloat16),
             pltpu.VMEM((SPANS, 1, tokens), jnp.int32),
             dma((5,)),
+            pltpu.VMEM((2, 2, tokens, HD), jnp.bfloat16),
+            pltpu.VMEM((2, tokens, HD), jnp.bfloat16),
+            dma((2, 2)),
+            dma((2, 2)),
+            dma((2,)),
+            dma((2,)),
             dma((3, SPANS - 1)),
             dma((3, SPANS - 1)),
             dma((2, seq_devices)),

time: 66.5 us -> 64.6 us (0.971); the launches traced: 65.4 us -> 64.5 us
  Pallas kernels: 64.8 us -> 63.9 us
    pallas_call x1, Pallas kernels: 53.3 us -> 52.4 us  [on_device(): pl.pallas_call(functools.partial(exchange_kernel, seq_devices, head_devic...]
where the time goes in v4:
time: 64.6 us; the launch traced here: 64.5 us
  Pallas kernels  63.9 us (99%)
    pallas_call x1, Pallas kernels, on_device(): pl.pallas_call(functools.partial(exchange_kernel, seq_devices, head_devic...  52.4 us
    pallas_call x1, Pallas kernels, on_device(): pl.pallas_call(hessian_kernel, out_shape=(jax.ShapeDtypeStruct((tokens, w...  11.5 us

profile of v4, /device:TPU:25, one launch (start us, length us, event | category | flops | bytes accessed | tf_op | source)
XLA Modules:
  0.0 64.5 jit_solution(7926913433300155442)
XLA Ops:
  0.6 52.4 %attend_exchange.1 = (bf16[128,2048]{1,0:T(8,128)(2,1)S(1)}, bf16[2048,512]{1,0:T(8,128)(2,1)S(1)}, bf16[512,4096]{1,0:T(8,128)(2,1)S(1)}) custom-call(bf16[128,2048]{1,0:T(8,128)(2,1)} %q_hbm.1, bf16[128,1024]{1,0:T(8,128)(2,1)} %k_hbm.1, bf16[128,1024]{1,0:T(8,128)(2,1)} %v_hbm.1, s32[1,128]{1,0:T(1,128)} %bitcast.1), custom_call_target="tpu_custom_call" | custom-call | tf_op jit(solution)/shard_map/attend_exchange/pallas_call | solution.py:646
  53.0 11.5 %hessian.1 = (bf16[128,2048]{1,0:T(8,128)(2,1)}, f32[2048,4096]{1,0:T(8,128)}) custom-call(bf16[128,2048]{1,0:T(8,128)(2,1)S(1)} %get-tuple-element.5.own_ref, bf16[2048,512]{1,0:T(8,128)(2,1)S(1)} %get-tuple-element.6.turned_ref, bf16[512,4096]{1,0:T(8,128)(2,1)S(1)} %get-tuple-element.7.cols_ref), custom_call_target="tpu_custom_call" | custom-call | tf_op jit(solution)/shard_map/hessian/pallas_call | solution.py:688

commit v5 on v4

--- a/solution.py
+++ b/solution.py
@@ -17,8 +17,8 @@
 MIDDLE_LEAD = 1
 LAG_ONE = 1
 LAG_TWO = 3
-LAG_THREE = 5
-RAW_PAIRS = 1
+LAG_THREE = 6
+RAW_PAIRS = 2
 TILE = 512
 PIECES = 4
 SLOTS = 4
@@ -30,7 +30,7 @@
     seq_devices, head_devices, chunks, raw_pairs,
     q_hbm, k_hbm, v_hbm, pos_hbm, attended_ref, turned_ref, cols_ref,
     q_ref, raw_ref, rows_ref, kbuf, vbuf, pbuf,
-    load_sems, detour, landed, detour_load, detour_send, detour_recv, onward_send, kv_send, kv_recv, line_send, line_recv, tree_send, tree_recv, lane_send, lane_recv,
+    load_sems, detour, landed, detour_load, detour_send, detour_recv, onward_send, kv_send, kv_recv, line_send, line_recv, tree_send, tree_recv, corner_send, lane_send, lane_recv,
 ):
     tokens, width = q_ref.shape
     lanes = head_devices // seq_devices
@@ -257,6 +257,13 @@
             src_ref=source, dst_ref=cols_ref.at[col_chunk(lane, block, part)],
             send_sem=tree_send.at[bit, kind, turn, block], recv_sem=tree_recv.at[block, part],
             device_id={"head": flip(bit)}, device_id_type=MESH,
+        )
+
+    def corner_copy(block, source):
+        return pltpu.make_async_remote_copy(
+            src_ref=source, dst_ref=cols_ref.at[col_chunk(lane, block, chunks - 1)],
+            send_sem=corner_send.at[block], recv_sem=tree_recv.at[block, chunks - 1],
+            device_id={"head": across(2**bits - 1)}, device_id_type=MESH,
         )
 
     def lane_copy(step, of_lane, block, part, source):
@@ -288,20 +295,27 @@
             for depth in depths
         ]
         tree_lag = jnp.where(tree_depth == 1, LAG_ONE, LAG_TWO)
-        longest = LAG_THREE
         kinds = 2
     else:
         walk_now = tree_now
         lags = [LAG_ONE * tree_depth] * 2
-        longest = LAG_ONE * bits
         kinds = 1
 
     def share(turn, block, part, source, kind):
         now = tree_now if kind else walk_now
+        straight = shifted and kind == 1 and turn == 1
         for bit in range(bits):
-            @pl.when(now[turn][bit])
+            needed = now[turn][bit]
+            if straight:
+                needed = jnp.logical_and(needed, jnp.logical_or(root, part != chunks - 1))
+
+            @pl.when(needed)
             def _():
                 tree_copy(bit, kind, turn, block, part, source).start()
+        if straight:
+            @pl.when(jnp.logical_and(root, part == chunks - 1))
+            def _():
+                corner_copy(block, source).start()
         for step in range(1, lanes):
             lane_copy(step, lane, block, part, source).start()
 
@@ -467,8 +481,10 @@
         def _():
             act(span + distance)
 
+    lead = jnp.where(at_end, LEAD, MIDDLE_LEAD)
+
     def behind(item, lag):
-        late = item - jnp.where(at_end, LEAD, MIDDLE_LEAD) - lag
+        late = item - lead - lag
         distance = lax.div(jnp.maximum(late, 0), pairs)
         pair = jnp.maximum(late, 0) - distance * pairs
         if raw_pairs:
@@ -521,9 +537,19 @@
         walk(item)
         return carry
 
-    lax.fori_loop(0, pairs, late_walk, 0)
-    lax.fori_loop(pairs, seq_devices * pairs, relay, 0)
-    lax.fori_loop(seq_devices * pairs, seq_devices * pairs + max(LEAD, MIDDLE_LEAD) + longest, late_walk, 0)
+    total = seq_devices * pairs
+    longest = jnp.maximum(lags[0], lags[1])
+    if kinds == 2:
+        final_lag = jnp.maximum(tree_lag, longest - pairs)
+        first_lag = jnp.minimum(lags[0], lags[1])
+    else:
+        final_lag = longest
+        first_lag = longest
+    begin = jnp.where(root, pairs, jnp.minimum(lead + first_lag, pairs))
+    trailing = jnp.where(root, 0, lead + final_lag)
+    lax.fori_loop(begin, pairs, late_walk, 0)
+    lax.fori_loop(pairs, total, relay, 0)
+    lax.fori_loop(total, total + trailing, late_walk, 0)
 
     def sized(rows, columns, send, recv):
         view = rows_ref.at[pl.ds(0, rows), pl.ds(0, columns)]
@@ -546,9 +572,9 @@
         final = jnp.abs(block - span) == farthest
         for bit in range(bits):
             for turn in range(2):
-                def wait_tree(kind):
+                def wait_tree(kind, count=pairs):
                     sized(
-                        tokens, pairs * chunk_width, tree_send.at[bit, kind, turn, block], spare
+                        tokens, count * chunk_width, tree_send.at[bit, kind, turn, block], spare
                     ).wait_send()
 
                 if kinds == 2:
@@ -556,13 +582,27 @@
                     def _():
                         wait_tree(0)
 
-                    @pl.when(jnp.logical_and(tree_now[turn][bit], final))
+                    relays = tree_now[turn][bit]
+                    if shifted and turn == 1:
+                        if pairs > 1:
+                            @pl.when(jnp.logical_and(jnp.logical_and(relays, final), not_root))
+                            def _():
+                                wait_tree(1, pairs - 1)
+
+                        relays = jnp.logical_and(relays, root)
+
+                    @pl.when(jnp.logical_and(relays, final))
                     def _():
                         wait_tree(1)
                 else:
                     @pl.when(walk_now[turn][bit])
                     def _():
                         wait_tree(0)
+        if shifted:
+            @pl.when(jnp.logical_and(root, final))
+            def _():
+                sized(tokens, chunk_width, corner_send.at[block], spare).wait_send()
+
         for step in range(1, lanes):
             whole = sized(
                 tokens, width, lane_send.at[step - 1, block], lane_recv.at[step - 1, block]
@@ -674,6 +714,7 @@
             dma((seq_devices, chunks)),
             dma((bits, 2 if bits == 2 else 1, 2, seq_devices)),
             dma((seq_devices, chunks)),
+            dma((seq_devices,)),
             dma((lanes - 1, seq_devices)),
             dma((lanes - 1, seq_devices)),
         ],

time: 64.6 us -> 63.4 us (0.981)
  Pallas kernels: 63.9 us -> 62.4 us
    pallas_call x1, Pallas kernels: 52.4 us -> 51 us  [on_device(): pl.pallas_call(functools.partial(exchange_kernel, seq_devices, head_devic...]
where the time goes in v5:
time: 63.4 us; the launch traced here: 63.1 us
  Pallas kernels  62.4 us (98%)
  between operations  0.64 us (1%)
    pallas_call x1, Pallas kernels, on_device(): pl.pallas_call(functools.partial(exchange_kernel, seq_devices, head_devic...  51 us
    pallas_call x1, Pallas kernels, on_device(): pl.pallas_call(hessian_kernel, out_shape=(jax.ShapeDtypeStruct((tokens, w...  11.5 us

profile of v5, /device:TPU:25, one launch (start us, length us, event | category | flops | bytes accessed | tf_op | source)
XLA Modules:
  0.0 63.1 jit_solution(4835845531799095949)
XLA Ops:
  0.6 51.0 %attend_exchange.1 = (bf16[128,2048]{1,0:T(8,128)(2,1)S(1)}, bf16[2048,512]{1,0:T(8,128)(2,1)S(1)}, bf16[512,4096]{1,0:T(8,128)(2,1)S(1)}) custom-call(bf16[128,2048]{1,0:T(8,128)(2,1)} %q_hbm.1, bf16[128,1024]{1,0:T(8,128)(2,1)} %k_hbm.1, bf16[128,1024]{1,0:T(8,128)(2,1)} %v_hbm.1, s32[1,128]{1,0:T(1,128)} %bitcast.1), custom_call_target="tpu_custom_call" | custom-call | tf_op jit(solution)/shard_map/attend_exchange/pallas_call | solution.py:686
  51.6 11.5 %hessian.1 = (bf16[128,2048]{1,0:T(8,128)(2,1)}, f32[2048,4096]{1,0:T(8,128)}) custom-call(bf16[128,2048]{1,0:T(8,128)(2,1)S(1)} %get-tuple-element.5.own_ref, bf16[2048,512]{1,0:T(8,128)(2,1)S(1)} %get-tuple-element.6.turned_ref, bf16[512,4096]{1,0:T(8,128)(2,1)S(1)} %get-tuple-element.7.cols_ref), custom_call_target="tpu_custom_call" | custom-call | tf_op jit(solution)/shard_map/hessian/pallas_call | solution.py:729
